TPU v7x, 32 devices: a whole 2x2x4 slice. The times are simulated.
32 devices in a mesh: seq: 8 (over z, x), tensor: 4 (over y, core).
Axes of the slice: x: 2, y: 2, z: 4, core: 2. Of those that a mesh axis runs over, the one named last changes fastest.
Arguments:
- tokens: bfloat16 [4096, 2048], P('seq', 'tensor'), may hold values from -12 to 12
- attn_gain: float32 [2048], replicated, may hold values from 0.1 to 1.9
- w_query: bfloat16 [2048, 2048], P('seq', 'tensor'), as said below
- w_key: bfloat16 [2048, 512], P('seq', 'tensor'), as said below
- w_value: bfloat16 [2048, 512], P('seq', 'tensor'), may hold values from -0.125 to 0.125
- w_out: bfloat16 [2048, 2048], P('tensor', 'seq'), may hold values from -0.125 to 0.125
- mlp_gain: float32 [2048], replicated, may hold values from 0.1 to 1.9
- w_gate: bfloat16 [2048, 5632], P('seq', 'tensor'), may hold values from -0.125 to 0.125
- w_up: bfloat16 [2048, 5632], P('seq', 'tensor'), may hold values from -0.125 to 0.125
- w_down: bfloat16 [5632, 2048], P('tensor', 'seq'), may hold values from -0.078125 to 0.078125
Outputs:
- layer_out: bfloat16 [4096, 2048], P('seq', 'tensor')
Inputs may be any that keep to these rules, and one draw needn't show every extreme that they name: `w_query`: entries are of order 2048 to the power -1/2. `w_key`: entries are of order 2048 to the power -1/2.
All inputs are finite; a program needn't handle non-finite values.
Results may differ from a plain program's by a relative error of at most 0.013.
Values may be sent and summed in bfloat16 or wider, within the bound.
A program may use at most 128 MiB of HBM per device.

v0:
```python
import jax
import jax.numpy as jnp
from jax import lax
from jax.sharding import PartitionSpec as P

HEAD_DIM = 128
WINDOW = 1024


def passed_along(block, axis, distance):
    devices = range(lax.axis_size(axis))
    route = [(i - distance, i) for i in devices if i - distance in devices]
    return lax.ppermute(block, axis, route)


def scaled_rows(values, gain):
    values = values.astype(jnp.float32)
    mean_square = jnp.mean(values * values, axis=1, keepdims=True)
    return (values * lax.rsqrt(mean_square + 1e-06) * gain).astype(jnp.bfloat16)


def product(left, right):
    return jnp.dot(left, right, preferred_element_type=jnp.float32)


def window_attention(queries, context_keys, context_values, reach, position):
    rows = queries.shape[0]
    local_kv = context_keys.shape[1] // HEAD_DIM
    group = queries.shape[1] // (local_kv * HEAD_DIM)
    block = min(512, rows)
    span = WINDOW + block
    scale = HEAD_DIM ** (-0.5)
    start = reach * rows - WINDOW
    query_block = queries.reshape(block, local_kv, group, HEAD_DIM)
    key_block = context_keys.reshape(span, local_kv, HEAD_DIM)
    value_block = context_values.reshape(span, local_kv, HEAD_DIM)
    scores = (
        jnp.einsum("qkgd,ckd->kgqc", query_block, key_block, preferred_element_type=jnp.float32)
        * scale
    )
    query_pos = lax.broadcasted_iota(jnp.int32, (block, span), 0)
    key_pos = lax.broadcasted_iota(jnp.int32, (block, span), 1)
    distance = query_pos + WINDOW - key_pos
    first_key = (position - reach) * rows + start
    allowed = (distance >= 0) & (distance < WINDOW) & (key_pos + first_key >= 0)
    scores = jnp.where(allowed[None, None], scores, -1e30)
    highest = jnp.max(scores, axis=3, keepdims=True)
    raised = jnp.exp(scores - highest)
    weights = (raised / jnp.sum(raised, axis=3, keepdims=True)).astype(jnp.bfloat16)
    mixed = jnp.einsum("kgqc,ckd->qkgd", weights, value_block, preferred_element_type=jnp.float32)
    outputs = mixed.astype(jnp.bfloat16).reshape(block, local_kv * group * HEAD_DIM)
    return outputs


def per_device(tokens, attn_gain, w_query, w_key, w_value, w_out, mlp_gain, w_gate, w_up, w_down):
    rows = tokens.shape[0]
    whole = lax.all_gather(tokens, "tensor", axis=1, tiled=True)
    normed = scaled_rows(whole, attn_gain)
    query_full = lax.all_gather(w_query, "seq", axis=0, tiled=True)
    key_full, value_full = (
        lax.all_gather(w_key, "seq", axis=0, tiled=True),
        lax.all_gather(w_value, "seq", axis=0, tiled=True),
    )
    queries = product(normed, query_full).astype(jnp.bfloat16)
    keys = product(normed, key_full).astype(jnp.bfloat16)
    values = product(normed, value_full).astype(jnp.bfloat16)
    reach = -(-WINDOW // rows)
    earlier = []
    for step in range(reach):
        earlier.append(passed_along((keys, values), "seq", step + 1))
    context_keys = jnp.concatenate(
        [earlier[reach - 1 - step][0] for step in range(reach)] + [keys], axis=0
    )
    context_values = jnp.concatenate(
        [earlier[reach - 1 - step][1] for step in range(reach)] + [values], axis=0
    )
    position = lax.axis_index("seq")
    attended = window_attention(queries, context_keys, context_values, reach, position)
    out_full = lax.all_gather(w_out, "seq", axis=1, tiled=True)
    head_terms = product(attended, out_full)
    share = tokens.shape[1]
    attn_whole = lax.psum(head_terms.astype(jnp.bfloat16), "tensor").astype(jnp.float32)
    stream_whole = (whole.astype(jnp.float32) + attn_whole).astype(jnp.bfloat16)
    stream_share = lax.dynamic_slice_in_dim(
        stream_whole, lax.axis_index("tensor") * share, share, 1
    )
    stream_normed = scaled_rows(stream_whole, mlp_gain)
    gate_full = lax.all_gather(w_gate, "seq", axis=0, tiled=True)
    up_full = lax.all_gather(w_up, "seq", axis=0, tiled=True)
    gate = product(stream_normed, gate_full)
    upward = product(stream_normed, up_full)
    hidden = (jax.nn.silu(gate) * upward).astype(jnp.bfloat16)
    down_full = lax.all_gather(w_down, "seq", axis=1, tiled=True)
    unit_terms = product(hidden, down_full)
    mlp_share = lax.psum_scatter(
        unit_terms.astype(jnp.bfloat16), "tensor", scatter_dimension=1, tiled=True
    ).astype(jnp.float32)
    return (stream_share.astype(jnp.float32) + mlp_share).astype(jnp.bfloat16)


def solution(mesh):
    in_specs = (
        P("seq", "tensor"),
        P(),
        P("seq", "tensor"),
        P("seq", "tensor"),
        P("seq", "tensor"),
        P("tensor", "seq"),
        P(),
        P("seq", "tensor"),
        P("seq", "tensor"),
        P("tensor", "seq"),
    )
    out_specs = P("seq", "tensor")
    return jax.shard_map(
        per_device, mesh=mesh, in_specs=in_specs, out_specs=out_specs, check_vma=False
    )
```

profile of v0, /device:TPU:0, one launch (start us, length us, event | category | flops | bytes accessed | tf_op | source)
XLA Modules:
  0.0 529.0 jit_solution(15447656682437301794)
XLA Ops:
  6.5 0.7 all-gather.7.cloned.1.call-update
  7.3 0.0 all-gather.9.cloned.1.call-start
  7.3 0.7 all-gather.9.cloned.1.call-update
  8.0 0.0 all-gather.11.cloned.1.call-start
  8.1 0.7 all-gather.11.cloned.1.call-update
  8.7 0.0 all-reduce.2.cloned.1.call-start
  8.8 33.4 %all_gather.26 = bf16[2048,128]{1,0:T(8,128)(2,1)S(1)} all-gather(bf16[256,128]{1,0:T(8,128)(2,1)} %param.13), channel_id=1, replica_groups=mesh['seq'=8,'tensor'=4] {'seq'}, dimensions={0}, use_global_device_ids=true | all-gather | bytes 589824 | tf_op jit(solution)/shard_map/all_gather | solution.py:61
  42.2 35.2 %all_gather.25 = bf16[2048,128]{1,0:T(8,128)(2,1)} all-gather(bf16[256,128]{1,0:T(8,128)(2,1)} %param.14), channel_id=1, replica_groups=mesh['seq'=8,'tensor'=4] {'seq'}, dimensions={0}, use_global_device_ids=true | all-gather | bytes 589824 | tf_op jit(solution)/shard_map/all_gather | solution.py:62
  77.3 1.3 fusion.14
  78.6 0.0 all-gather.7.cloned.1.call-done
  78.7 2.2 fusion.7
  80.9 2.4 convolution_convert_fusion.3
  83.3 1.3 collective-permute-start.2
  84.6 4.3 collective-permute-start.3
  88.9 0.8 convolution_convert_fusion.4
  89.6 2.7 collective-permute-start
  92.4 2.7 collective-permute-start.1
  95.1 0.0 all-gather.9.cloned.1.call-done
  95.1 3.0 convolution_convert_fusion.2
  98.1 0.0 collective-permute-done.2
  98.1 0.0 collective-permute-done.3
  98.1 3.3 fusion.1
  101.4 2.8 fusion
  104.2 0.0 collective-permute-done
  104.2 0.0 collective-permute-done.1
  104.2 4.8 fusion.16
  109.0 33.7 %all-gather.11.cloned.1.call-done = bf16[512,2048]{1,0:T(8,128)(2,1)} async-done(((bf16[512,256]{1,0:T(8,128)(2,1)}), bf16[512,2048]{1,0:T(8,128)(2,1)}) %all-gather.11.cloned.1.call-update) | async-done | bytes 2097168 | tf_op jit(solution)/shard_map/all_gather | solution.py:79
  142.7 4.4 convolution_convert_fusion
  147.1 0.0 all-reduce.2.cloned.1.call-update
  147.1 0.0 copy-start.4
  147.1 0.0 all-gather.13.cloned.1.call-start
  147.2 0.5 all-gather.13.cloned.1.call-update
  147.7 0.0 all-gather.15.cloned.1.call-start
  147.8 0.5 all-gather.15.cloned.1.call-update
  148.3 0.0 all-gather.17.cloned.1.call-start
  148.4 0.7 all-gather.17.cloned.1.call-update
  149.1 0.3 reduce-scatter.2.cloned.1.call-start
  149.3 47.5 %all-reduce.2.cloned.1.call-done = bf16[512,2048]{1,0:T(8,128)(2,1)} async-done(((bf16[512,2048]{1,0:T(8,128)(2,1)}), bf16[512,2048]{1,0:T(8,128)(2,1)}) %all-reduce.2.cloned.1.call-update) | async-done | bytes 2097168 | tf_op jit(solution)/shard_map/psum | solution.py:82
  196.9 3.9 fusion.4
  200.8 90.5 %all-gather.13.cloned.1.call-done = bf16[2048,1408]{1,0:T(8,128)(2,1)} async-done(((bf16[256,1408]{1,0:T(8,128)(2,1)}), bf16[2048,1408]{1,0:T(8,128)(2,1)}) %all-gather.13.cloned.1.call-update) | async-done | bytes 5767184 | tf_op jit(solution)/shard_map/all_gather | solution.py:88
  291.3 8.4 %fusion.21 = f32[512,1408]{1,0:T(8,128)} fusion(bf16[2048,1408]{1,0:T(8,128)(2,1)} %all-gather.13.cloned.1.call-done, bf16[512,2048]{1,0:T(8,128)(2,1)} %get-tuple-element.6, f32[2048]{0:T(1024)S(1)} %copy-done.4, f32[512]{0:T(512)S(1)} %add_rsqrt_fusion), kind=kOutput, calls=%fused_computation.33 | convolution fusion | flops 2956984320 | bytes 10758144 | tf_op jit(solution)/shard_map/dot_general | solution.py:23
  299.7 84.1 %all-gather.15.cloned.1.call-done = bf16[2048,1408]{1,0:T(8,128)(2,1)} async-done(((bf16[256,1408]{1,0:T(8,128)(2,1)}), bf16[2048,1408]{1,0:T(8,128)(2,1)}) %all-gather.15.cloned.1.call-update) | async-done | bytes 5767184 | tf_op jit(solution)/shard_map/all_gather | solution.py:89
  383.9 93.4 %all-gather.17.cloned.1.call-done = bf16[1408,2048]{1,0:T(8,128)(2,1)} async-done(((bf16[1408,256]{1,0:T(8,128)(2,1)}), bf16[1408,2048]{1,0:T(8,128)(2,1)}) %all-gather.17.cloned.1.call-update) | async-done | bytes 5767184 | tf_op jit(solution)/shard_map/all_gather | solution.py:93
  477.2 0.0 copy-done.1
  477.2 13.4 %convolution_convert_fusion.1 = bf16[512,2048]{1,0:T(8,128)(2,1)} fusion(bf16[1408,2048]{1,0:T(8,128)(2,1)} %all-gather.17.cloned.1.call-done, bf16[2048,1408]{1,0:T(8,128)(2,1)} %all-gather.15.cloned.1.call-done, f32[512,1408]{1,0:T(8,128)} %fusion.21, bf16[512,2048]{1,0:T(8,128)(2,1)S(1)} %copy-done.1, f32[2048]{0:T(1024)S(1)} %copy-done.4, ...), kind=kOutput, calls=%fused_computation.27 | convolution fusion | flops 5915148288 | bytes 18622464 | tf_op jit(solution)/shard_map/dot_general | solution.py:23
  490.7 0.0 reduce-scatter.2.cloned.1.call-update
  490.7 29.5 %reduce-scatter.2.cloned.1.call-done = bf16[512,512]{1,0:T(8,128)(2,1)} async-done(((bf16[512,2048]{1,0:T(8,128)(2,1)}), bf16[512,512]{1,0:T(8,128)(2,1)}) %reduce-scatter.2.cloned.1.call-update) | async-done | bytes 524304 | tf_op jit(solution)/shard_map/reduce_scatter | solution.py:95
  520.2 2.0 add_convert_fusion
  (13 shorter events, 0.0 us)
Async XLA Ops:
  6.5 74.4 %copy-start.3 = (f32[2048]{0:T(1024)S(1)}, f32[2048]{0:T(1024)}, u32[]{:S(2)}) copy-start(f32[2048]{0:T(1024)} %param.11) | copy-start | bytes 24580
  6.5 72.1 %all-gather.7.cloned.1.call-start = ((), (), s32[]{:S(2)}) async-start(), calls=%async_computation.1 | async-start | bytes 2621440 | tf_op jit(solution)/shard_map/all_gather | solution.py:57
  7.3 87.8 %all-gather.9.cloned.1.call-start = ((), (), s32[]{:S(2)}) async-start(), calls=%async_computation.2 | async-start | bytes 2359296 | tf_op jit(solution)/shard_map/all_gather | solution.py:59
  8.0 134.7 %all-gather.11.cloned.1.call-start = ((), (), s32[]{:S(2)}) async-start(), calls=%async_computation.3 | async-start | bytes 2359296 | tf_op jit(solution)/shard_map/all_gather | solution.py:79
  8.7 188.1 %all-reduce.2.cloned.1.call-start = ((), (), s32[]{:S(2)}) async-start(), calls=%async_computation.4 | async-start | bytes 4194304 | tf_op jit(solution)/shard_map/psum | solution.py:82
  78.6 10.2 %copy-start = (bf16[512,2048]{1,0:T(8,128)(2,1)S(1)}, bf16[512,2048]{1,0:T(8,128)(2,1)}, u32[]{:S(2)}) copy-start(bf16[512,2048]{1,0:T(8,128)(2,1)} %all-gather.7.cloned.1.call-done) | copy-start | bytes 6291460
  78.7 10.2 %copy-start.2 = (bf16[2048,128]{1,0:T(8,128)(2,1)S(1)}, bf16[2048,128]{1,0:T(8,128)(2,1)}, u32[]{:S(2)}) copy-start(bf16[2048,128]{1,0:T(8,128)(2,1)} %all_gather.25) | copy-start | bytes 1572868
  83.3 14.8 %collective-permute-start.2 = (bf16[512,128]{1,0:T(8,128)(2,1)S(1)}, bf16[512,128]{1,0:T(8,128)(2,1)S(1)}, u32[]{:S(2)}, u32[]{:S(2)}) collective-permute-start(bf16[512,128]{1,0:T(8,128)(2,1)S(1)} %convolution_convert_fusion.3), channel_id=1, source_target_pairs={{0,8},{4,12},{8,16},{12,20},{16,24},{20,28},{1,9},{5,13},{9,17},{1... | collective-permute-start | bytes 393224 | tf_op jit(solution)/shard_map/ppermute | solution.py:13
  84.6 13.5 %collective-permute-start.3 = (bf16[512,128]{1,0:T(8,128)(2,1)S(1)}, bf16[512,128]{1,0:T(8,128)(2,1)}, u32[]{:S(2)}, u32[]{:S(2)}) collective-permute-start(bf16[512,128]{1,0:T(8,128)(2,1)S(1)} %convolution_convert_fusion.3), channel_id=1, source_target_pairs={{0,4},{4,8},{8,12},{12,16},{16,20},{20,24},{24,28},{1,5},{5,9},{9,... | collective-permute-start | bytes 393224 | tf_op jit(solution)/shard_map/ppermute | solution.py:13
  89.6 14.5 %collective-permute-start = (bf16[512,128]{1,0:T(8,128)(2,1)S(1)}, bf16[512,128]{1,0:T(8,128)(2,1)S(1)}, u32[]{:S(2)}, u32[]{:S(2)}) collective-permute-start(bf16[512,128]{1,0:T(8,128)(2,1)S(1)} %convolution_convert_fusion.4), channel_id=1, source_target_pairs={{0,8},{4,12},{8,16},{12,20},{16,24},{20,28},{1,9},{5,13},{9,17},{1... | collective-permute-start | bytes 393224 | tf_op jit(solution)/shard_map/ppermute | solution.py:13
  92.4 11.8 %collective-permute-start.1 = (bf16[512,128]{1,0:T(8,128)(2,1)S(1)}, bf16[512,128]{1,0:T(8,128)(2,1)S(1)}, u32[]{:S(2)}, u32[]{:S(2)}) collective-permute-start(bf16[512,128]{1,0:T(8,128)(2,1)S(1)} %convolution_convert_fusion.4), channel_id=1, source_target_pairs={{0,4},{4,8},{8,12},{12,16},{16,20},{20,24},{24,28},{1,5},{5,9},{9,... | collective-permute-start | bytes 393224 | tf_op jit(solution)/shard_map/ppermute | solution.py:13
  147.1 144.2 %copy-start.4 = (f32[2048]{0:T(1024)S(1)}, f32[2048]{0:T(1024)}, u32[]{:S(2)}) copy-start(f32[2048]{0:T(1024)} %param.16) | copy-start | bytes 24580
  147.1 144.1 %all-gather.13.cloned.1.call-start = ((), (), s32[]{:S(2)}) async-start(), calls=%async_computation.5 | async-start | bytes 6488064 | tf_op jit(solution)/shard_map/all_gather | solution.py:88
  147.7 236.1 %all-gather.15.cloned.1.call-start = ((), (), s32[]{:S(2)}) async-start(), calls=%async_computation.6 | async-start | bytes 6488064 | tf_op jit(solution)/shard_map/all_gather | solution.py:89
  148.3 328.9 %all-gather.17.cloned.1.call-start = ((), (), s32[]{:S(2)}) async-start(), calls=%async_computation.7 | async-start | bytes 6488064 | tf_op jit(solution)/shard_map/all_gather | solution.py:93
  149.1 371.1 %reduce-scatter.2.cloned.1.call-start = ((), (), s32[]{:S(2)}) async-start(), calls=%async_computation.8 | async-start | bytes 2621440 | tf_op jit(solution)/shard_map/reduce_scatter | solution.py:95
  291.3 185.9 %copy-start.1 = (bf16[512,2048]{1,0:T(8,128)(2,1)S(1)}, bf16[512,2048]{1,0:T(8,128)(2,1)}, u32[]{:S(2)}) copy-start(bf16[512,2048]{1,0:T(8,128)(2,1)} %get-tuple-element.6) | copy-start | bytes 6291460
Sparse Core Ops, SparseCore 0:
  8.9 25.2 all-gather.6
  36.3 52.5 all-gather.8
  91.0 51.7 all-gather.10
  147.3 49.5 all-reduce.1
  198.9 92.3 all-gather.12
  293.3 90.4 all-gather.14
  385.9 91.2 all-gather.16
  490.8 29.3 reduce-scatter.1
where the time goes:
time: 529 us
  waiting for transfers between devices  383 us (72%)
  blocking collectives  68.5 us (13%)
  matrix products  40.5 us (8%)
  between operations  13.7 us (3%)
  other arithmetic  12.2 us (2%)
  starting transfers between devices  11.5 us (2%)
    all_gather x1, waiting for transfers between devices, per_device(): down_full = lax.all_gather(w_down, 'seq', axis=1, tiled=True)  93.4 us
    all_gather x1, waiting for transfers between devices, per_device(): gate_full = lax.all_gather(w_gate, 'seq', axis=0, tiled=True)  90.5 us
    all_gather x1, waiting for transfers between devices, per_device(): up_full = lax.all_gather(w_up, 'seq', axis=0, tiled=True)  84.1 us
    psum x1, waiting for transfers between devices, per_device(): lax.psum(head_terms.astype(jnp.bfloat16), 'tensor').astype(jnp.float32)  47.5 us
    all_gather x1, blocking collectives, per_device(): lax.all_gather(w_value, 'seq', axis=0, tiled=True)  35.2 us
    all_gather x1, waiting for transfers between devices, per_device(): out_full = lax.all_gather(w_out, 'seq', axis=1, tiled=True)  33.7 us
    all_gather x1, blocking collectives, per_device(): lax.all_gather(w_key, 'seq', axis=0, tiled=True)  33.4 us
    dot_general x6, matrix products, product(): return jnp.dot(left, right, preferred_element_type=jnp.float32)  32.3 us
  transfers between devices with their start and end apart: 12, of which 6 were waited for; matrix products, arithmetic and copies ran while one was open for 6% of the time, Pallas kernels for 0%

commit v1 on v0

--- a/solution.py
+++ b/solution.py
@@ -79,7 +79,9 @@
     out_full = lax.all_gather(w_out, "seq", axis=1, tiled=True)
     head_terms = product(attended, out_full)
     share = tokens.shape[1]
-    attn_whole = lax.psum(head_terms.astype(jnp.bfloat16), "tensor").astype(jnp.float32)
+    attn_whole = jnp.sum(lax.all_gather(head_terms.astype(jnp.bfloat16), "tensor"), axis=0).astype(
+        jnp.float32
+    )
     stream_whole = (whole.astype(jnp.float32) + attn_whole).astype(jnp.bfloat16)
     stream_share = lax.dynamic_slice_in_dim(
         stream_whole, lax.axis_index("tensor") * share, share, 1

time: 529 us -> 536 us (1.013)
  other arithmetic: 12.2 us -> 19.4 us
    all_gather x0 -> x1, waiting for transfers between devices: none -> 54.4 us  [per_device(): lax.all_gather(head_terms.astype(jnp.bfloat16), 'tensor')]
    psum x1 -> x0, waiting for transfers between devices: 47.5 us -> none  [per_device(): lax.psum(head_terms.astype(jnp.bfloat16), 'tensor').astype(jnp.float32)]
    all_gather x1, waiting for transfers between devices: 90.5 us -> 83.3 us  [per_device(): gate_full = lax.all_gather(w_gate, 'seq', axis=0, tiled=True)]
    reduce_sum x0 -> x1, other arithmetic: none -> 7.19 us  [per_device(): jnp.sum(lax.all_gather(head_terms.astype(jnp.bfloat16), 'tensor'), axis=0)]
  transfers between devices with their start and end apart: 12 -> 12, of which waited for: 6 -> 6; matrix products, arithmetic and copies ran while one was open for 6% -> 7% of each run, Pallas kernels for 0% -> 0%
where the time goes in v1:
time: 536 us
  waiting for transfers between devices  382 us (71%)
  blocking collectives  68.5 us (13%)
  matrix products  40.4 us (8%)
  other arithmetic  19.4 us (4%)
  between operations  13.6 us (3%)
  starting transfers between devices  11.5 us (2%)
    all_gather x1, waiting for transfers between devices, per_device(): down_full = lax.all_gather(w_down, 'seq', axis=1, tiled=True)  93.4 us
    all_gather x1, waiting for transfers between devices, per_device(): up_full = lax.all_gather(w_up, 'seq', axis=0, tiled=True)  84.1 us
    all_gather x1, waiting for transfers between devices, per_device(): gate_full = lax.all_gather(w_gate, 'seq', axis=0, tiled=True)  83.3 us
    all_gather x1, waiting for transfers between devices, per_device(): lax.all_gather(head_terms.astype(jnp.bfloat16), 'tensor')  54.4 us
    all_gather x1, blocking collectives, per_device(): lax.all_gather(w_value, 'seq', axis=0, tiled=True)  35.1 us
    all_gather x1, waiting for transfers between devices, per_device(): out_full = lax.all_gather(w_out, 'seq', axis=1, tiled=True)  33.7 us
    all_gather x1, blocking collectives, per_device(): lax.all_gather(w_key, 'seq', axis=0, tiled=True)  33.4 us
    dot_general x6, matrix products, product(): return jnp.dot(left, right, preferred_element_type=jnp.float32)  32.3 us
  transfers between devices with their start and end apart: 12, of which 6 were waited for; matrix products, arithmetic and copies ran while one was open for 7% of the time, Pallas kernels for 0%

profile of v1, /device:TPU:0, one launch (start us, length us, event | category | flops | bytes accessed | tf_op | source)
XLA Modules:
  0.0 535.7 jit_solution(16254875460456056541)
XLA Ops:
  6.5 0.0 all-gather.9.cloned.1.call-start
  6.5 0.7 all-gather.9.cloned.1.call-update
  7.3 0.0 all-gather.11.cloned.1.call-start
  7.3 0.7 all-gather.11.cloned.1.call-update
  8.0 0.0 all-gather.13.cloned.1.call-start
  8.1 0.7 all-gather.13.cloned.1.call-update
  8.7 0.0 all-gather.21.cloned.1.call-start
  8.8 33.4 %all_gather.32 = bf16[2048,128]{1,0:T(8,128)(2,1)S(1)} all-gather(bf16[256,128]{1,0:T(8,128)(2,1)} %param.13), channel_id=1, replica_groups=mesh['seq'=8,'tensor'=4] {'seq'}, dimensions={0}, use_global_device_ids=true | all-gather | bytes 589824 | tf_op jit(solution)/shard_map/all_gather | solution.py:61
  42.2 35.1 %all_gather.31 = bf16[2048,128]{1,0:T(8,128)(2,1)} all-gather(bf16[256,128]{1,0:T(8,128)(2,1)} %param.14), channel_id=1, replica_groups=mesh['seq'=8,'tensor'=4] {'seq'}, dimensions={0}, use_global_device_ids=true | all-gather | bytes 589824 | tf_op jit(solution)/shard_map/all_gather | solution.py:62
  77.3 1.3 fusion.14
  78.6 0.0 all-gather.9.cloned.1.call-done
  78.7 2.2 fusion.7
  80.9 2.4 convolution_convert_fusion.3
  83.3 1.3 collective-permute-start.2
  84.6 4.3 collective-permute-start.3
  88.9 0.8 convolution_convert_fusion.4
  89.6 2.7 collective-permute-start
  92.4 2.7 collective-permute-start.1
  95.1 0.0 all-gather.11.cloned.1.call-done
  95.1 3.0 convolution_convert_fusion.2
  98.1 0.0 collective-permute-done.2
  98.1 0.0 collective-permute-done.3
  98.1 3.3 fusion.1
  101.4 2.8 fusion
  104.2 0.0 collective-permute-done
  104.2 0.0 collective-permute-done.1
  104.2 4.8 fusion.16
  109.0 33.7 %all-gather.13.cloned.1.call-done = bf16[512,2048]{1,0:T(8,128)(2,1)} async-done(((bf16[512,256]{1,0:T(8,128)(2,1)}), bf16[512,2048]{1,0:T(8,128)(2,1)}) %all-gather.13.cloned.1.call-update) | async-done | bytes 2097168 | tf_op jit(solution)/shard_map/all_gather | solution.py:79
  142.8 4.4 convolution_convert_fusion
  147.1 0.0 all-gather.21.cloned.1.call-update
  147.2 0.0 all-gather.15.cloned.1.call-start
  147.2 0.5 all-gather.15.cloned.1.call-update
  147.7 0.0 all-gather.17.cloned.1.call-start
  147.8 0.5 all-gather.17.cloned.1.call-update
  148.3 0.0 all-gather.19.cloned.1.call-start
  148.4 0.7 all-gather.19.cloned.1.call-update
  149.1 0.3 reduce-scatter.2.cloned.1.call-start
  149.3 54.4 %all-gather.21.cloned.1.call-done = bf16[2048,2048]{1,0:T(8,128)(2,1)} async-done(((bf16[512,2048]{1,0:T(8,128)(2,1)}), bf16[2048,2048]{1,0:T(8,128)(2,1)}) %all-gather.21.cloned.1.call-update) | async-done | bytes 8388624 | tf_op jit(solution)/shard_map/all_gather | solution.py:82
  203.8 7.2 %reduce_sum.41 = bf16[512,2048]{1,0:T(8,128)(2,1)} reduce(bf16[4,512,2048]{2,1,0:T(8,128)(2,1)} %bitcast.44, bf16[]{:T(256)} %constant.36.clone.1), dimensions={0}, to_apply=%region_3.4 | reduce | flops 3145728 | bytes 10485762 | tf_op jit(solution)/shard_map/reduce_sum | solution.py:82
  211.0 3.9 fusion.4
  214.9 83.3 %all-gather.15.cloned.1.call-done = bf16[2048,1408]{1,0:T(8,128)(2,1)} async-done(((bf16[256,1408]{1,0:T(8,128)(2,1)}), bf16[2048,1408]{1,0:T(8,128)(2,1)}) %all-gather.15.cloned.1.call-update) | async-done | bytes 5767184 | tf_op jit(solution)/shard_map/all_gather | solution.py:90
  298.1 8.4 %fusion.21 = f32[512,1408]{1,0:T(8,128)} fusion(bf16[2048,1408]{1,0:T(8,128)(2,1)} %all-gather.15.cloned.1.call-done, bf16[512,2048]{1,0:T(8,128)(2,1)} %get-tuple-element.6, f32[2048]{0:T(1024)S(1)} %copy-done.4, f32[512]{0:T(512)S(1)} %add_rsqrt_fusion), kind=kOutput, calls=%fused_computation.33 | convolution fusion | flops 2956984320 | bytes 10758144 | tf_op jit(solution)/shard_map/dot_general | solution.py:23
  306.6 84.1 %all-gather.17.cloned.1.call-done = bf16[2048,1408]{1,0:T(8,128)(2,1)} async-done(((bf16[256,1408]{1,0:T(8,128)(2,1)}), bf16[2048,1408]{1,0:T(8,128)(2,1)}) %all-gather.17.cloned.1.call-update) | async-done | bytes 5767184 | tf_op jit(solution)/shard_map/all_gather | solution.py:91
  390.7 93.4 %all-gather.19.cloned.1.call-done = bf16[1408,2048]{1,0:T(8,128)(2,1)} async-done(((bf16[1408,256]{1,0:T(8,128)(2,1)}), bf16[1408,2048]{1,0:T(8,128)(2,1)}) %all-gather.19.cloned.1.call-update) | async-done | bytes 5767184 | tf_op jit(solution)/shard_map/all_gather | solution.py:95
  484.1 13.3 %convolution_convert_fusion.1 = bf16[512,2048]{1,0:T(8,128)(2,1)} fusion(bf16[1408,2048]{1,0:T(8,128)(2,1)} %all-gather.19.cloned.1.call-done, bf16[2048,1408]{1,0:T(8,128)(2,1)} %all-gather.17.cloned.1.call-done, f32[512,1408]{1,0:T(8,128)} %fusion.21, bf16[512,2048]{1,0:T(8,128)(2,1)S(1)} %copy-done.1, f32[2048]{0:T(1024)S(1)} %copy-done.4, ...), kind=kOutput, calls=%fused_computation.27 | convolution fusion | flops 5915148288 | bytes 18622464 | tf_op jit(solution)/shard_map/dot_general | solution.py:23
  497.4 0.0 reduce-scatter.2.cloned.1.call-update
  497.4 29.5 %reduce-scatter.2.cloned.1.call-done = bf16[512,512]{1,0:T(8,128)(2,1)} async-done(((bf16[512,2048]{1,0:T(8,128)(2,1)}), bf16[512,512]{1,0:T(8,128)(2,1)}) %reduce-scatter.2.cloned.1.call-update) | async-done | bytes 524304 | tf_op jit(solution)/shard_map/reduce_scatter | solution.py:97
  526.9 2.0 add_convert_fusion
  (14 shorter events, 0.0 us)
Async XLA Ops:
  6.5 74.4 %copy-start.3 = (f32[2048]{0:T(1024)S(1)}, f32[2048]{0:T(1024)}, u32[]{:S(2)}) copy-start(f32[2048]{0:T(1024)} %param.11) | copy-start | bytes 24580
  6.5 72.1 %all-gather.9.cloned.1.call-start = ((), (), s32[]{:S(2)}) async-start(), calls=%async_computation.1 | async-start | bytes 2621440 | tf_op jit(solution)/shard_map/all_gather | solution.py:57
  7.3 87.8 %all-gather.11.cloned.1.call-start = ((), (), s32[]{:S(2)}) async-start(), calls=%async_computation.2 | async-start | bytes 2359296 | tf_op jit(solution)/shard_map/all_gather | solution.py:59
  8.0 134.8 %all-gather.13.cloned.1.call-start = ((), (), s32[]{:S(2)}) async-start(), calls=%async_computation.3 | async-start | bytes 2359296 | tf_op jit(solution)/shard_map/all_gather | solution.py:79
  8.7 195.0 %all-gather.21.cloned.1.call-start = ((), (), s32[]{:S(2)}) async-start(), calls=%async_computation.8 | async-start | bytes 10485760 | tf_op jit(solution)/shard_map/all_gather | solution.py:82
  78.6 10.2 %copy-start = (bf16[512,2048]{1,0:T(8,128)(2,1)S(1)}, bf16[512,2048]{1,0:T(8,128)(2,1)}, u32[]{:S(2)}) copy-start(bf16[512,2048]{1,0:T(8,128)(2,1)} %all-gather.9.cloned.1.call-done) | copy-start | bytes 6291460
  78.6 10.2 %copy-start.2 = (bf16[2048,128]{1,0:T(8,128)(2,1)S(1)}, bf16[2048,128]{1,0:T(8,128)(2,1)}, u32[]{:S(2)}) copy-start(bf16[2048,128]{1,0:T(8,128)(2,1)} %all_gather.31) | copy-start | bytes 1572868
  83.3 14.8 %collective-permute-start.2 = (bf16[512,128]{1,0:T(8,128)(2,1)S(1)}, bf16[512,128]{1,0:T(8,128)(2,1)S(1)}, u32[]{:S(2)}, u32[]{:S(2)}) collective-permute-start(bf16[512,128]{1,0:T(8,128)(2,1)S(1)} %convolution_convert_fusion.3), channel_id=1, source_target_pairs={{0,8},{4,12},{8,16},{12,20},{16,24},{20,28},{1,9},{5,13},{9,17},{1... | collective-permute-start | bytes 393224 | tf_op jit(solution)/shard_map/ppermute | solution.py:13
  84.6 13.5 %collective-permute-start.3 = (bf16[512,128]{1,0:T(8,128)(2,1)S(1)}, bf16[512,128]{1,0:T(8,128)(2,1)}, u32[]{:S(2)}, u32[]{:S(2)}) collective-permute-start(bf16[512,128]{1,0:T(8,128)(2,1)S(1)} %convolution_convert_fusion.3), channel_id=1, source_target_pairs={{0,4},{4,8},{8,12},{12,16},{16,20},{20,24},{24,28},{1,5},{5,9},{9,... | collective-permute-start | bytes 393224 | tf_op jit(solution)/shard_map/ppermute | solution.py:13
  89.6 14.5 %collective-permute-start = (bf16[512,128]{1,0:T(8,128)(2,1)S(1)}, bf16[512,128]{1,0:T(8,128)(2,1)S(1)}, u32[]{:S(2)}, u32[]{:S(2)}) collective-permute-start(bf16[512,128]{1,0:T(8,128)(2,1)S(1)} %convolution_convert_fusion.4), channel_id=1, source_target_pairs={{0,8},{4,12},{8,16},{12,20},{16,24},{20,28},{1,9},{5,13},{9,17},{1... | collective-permute-start | bytes 393224 | tf_op jit(solution)/shard_map/ppermute | solution.py:13
  92.4 11.8 %collective-permute-start.1 = (bf16[512,128]{1,0:T(8,128)(2,1)S(1)}, bf16[512,128]{1,0:T(8,128)(2,1)S(1)}, u32[]{:S(2)}, u32[]{:S(2)}) collective-permute-start(bf16[512,128]{1,0:T(8,128)(2,1)S(1)} %convolution_convert_fusion.4), channel_id=1, source_target_pairs={{0,4},{4,8},{8,12},{12,16},{16,20},{20,24},{24,28},{1,5},{5,9},{9,... | collective-permute-start | bytes 393224 | tf_op jit(solution)/shard_map/ppermute | solution.py:13
  147.2 151.0 %all-gather.15.cloned.1.call-start = ((), (), s32[]{:S(2)}) async-start(), calls=%async_computation.4 | async-start | bytes 6488064 | tf_op jit(solution)/shard_map/all_gather | solution.py:90
  147.7 242.9 %all-gather.17.cloned.1.call-start = ((), (), s32[]{:S(2)}) async-start(), calls=%async_computation.5 | async-start | bytes 6488064 | tf_op jit(solution)/shard_map/all_gather | solution.py:91
  148.3 335.8 %all-gather.19.cloned.1.call-start = ((), (), s32[]{:S(2)}) async-start(), calls=%async_computation.6 | async-start | bytes 6488064 | tf_op jit(solution)/shard_map/all_gather | solution.py:95
  149.1 377.8 %reduce-scatter.2.cloned.1.call-start = ((), (), s32[]{:S(2)}) async-start(), calls=%async_computation.7 | async-start | bytes 2621440 | tf_op jit(solution)/shard_map/reduce_scatter | solution.py:97
  211.0 87.2 %copy-start.4 = (f32[2048]{0:T(1024)S(1)}, f32[2048]{0:T(1024)}, u32[]{:S(2)}) copy-start(f32[2048]{0:T(1024)} %param.16) | copy-start | bytes 24580
  298.1 185.9 %copy-start.1 = (bf16[512,2048]{1,0:T(8,128)(2,1)S(1)}, bf16[512,2048]{1,0:T(8,128)(2,1)}, u32[]{:S(2)}) copy-start(bf16[512,2048]{1,0:T(8,128)(2,1)} %get-tuple-element.6) | copy-start | bytes 6291460
Sparse Core Ops, SparseCore 0:
  8.9 25.2 all-gather.8
  36.3 52.5 all-gather.10
  91.0 51.7 all-gather.12
  147.3 56.4 all-gather.20
  205.8 92.2 all-gather.14
  300.2 90.4 all-gather.16
  392.7 91.2 all-gather.18
  497.5 29.3 reduce-scatter.1
